TPU v7x, 32 devices: a whole 2x2x4 slice. The times are simulated.
32 devices in a mesh: gx: 2 (over core), gy: 16 (over z, y, x).
Axes of the slice: x: 2, y: 2, z: 4, core: 2. Of those that a mesh axis runs over, the one named last changes fastest.
Arguments:
- echoes: bfloat16 [32, 256, 16, 200], P('gx', 'gy'), may hold values from -6 to 6
- start: float32 [200, 32], replicated, may hold values from -6 to 6
- ranks: int32 [2, 16, 1], P('gx', 'gy'), may hold values from 2 to 32
- counts: int32 [2, 16, 1], P('gx', 'gy'), may hold values from 1 to 4
Outputs:
- filtered: bfloat16 [32, 256, 16, 200], P('gx', 'gy')
All inputs are finite; a program needn't handle non-finite values.
Results may differ from a plain program's by a relative error of at most 0.0075.
Values may be sent and summed in bfloat16 or wider, within the bound.
A program may use at most 128 MiB of HBM per device.

v0:
```python
import functools

import jax
import jax.numpy as jnp
from jax import lax
from jax.experimental import pallas as pl
from jax.experimental.pallas import tpu as pltpu
from jax.sharding import PartitionSpec as P

BZ = 16
ITERS = 4
LANES = 128
SUB = 8
GRANT = 16 << 20
MESH = pl.DeviceIdType.MESH


def tent(offset, span):
    inside = (offset >= 0.0) & (offset < span)
    return jnp.where(inside, 1.0 + jnp.minimum(offset, span - 1.0 - offset), 0.0)


def padded(size):
    return -(-size // LANES) * LANES


def row_of(tile, k):
    return jnp.broadcast_to(tile[k : k + 1, :], tile.shape)


def halves(x):
    high = x.astype(jnp.bfloat16)
    return high, (x - high.astype(jnp.float32)).astype(jnp.bfloat16)


def nt(a, b):
    return lax.dot_general(a, b, (((1,), (1,)), ((), ())), preferred_element_type=jnp.float32)


def orthonormal_rows(moved):
    size, width = moved.shape
    tiles = size // SUB
    high, low = halves(moved)
    inner = nt(high, high) + nt(low, high) + nt(high, low)
    columns = []
    for j in range(size):
        first = j // SUB
        columns.append(
            [
                jnp.broadcast_to(inner[SUB * i : SUB * i + SUB, j : j + 1], (SUB, LANES))
                for i in range(first, tiles)
            ]
        )
    rows = [
        [moved[SUB * i : SUB * i + SUB, LANES * h : LANES * h + LANES] for h in range(width // LANES)]
        for i in range(tiles)
    ]
    place = lax.broadcasted_iota(jnp.int32, (SUB, LANES), 0)
    scales = [None] * tiles
    for k in range(size):
        own, at = k // SUB, k % SUB
        root = lax.rsqrt(row_of(columns[k][0], at))
        scales[own] = root if at == 0 else jnp.where(place == at, root, scales[own])
        if k == size - 1:
            break
        inverse = root * root
        factor = [c * inverse for c in columns[k]]
        factor[0] = jnp.where(place > at, factor[0], 0.0)
        for j in range(k + 1, size):
            pivot = row_of(columns[k][j // SUB - own], j % SUB)
            shift = j // SUB - own
            columns[j] = [c - factor[i + shift] * pivot for i, c in enumerate(columns[j])]
        for h in range(width // LANES):
            pivot = row_of(rows[own][h], at)
            for i in range(own if at < SUB - 1 else own + 1, tiles):
                rows[i][h] = rows[i][h] - factor[i - own] * pivot
    return jnp.concatenate(
        [jnp.concatenate([part * scales[i] for part in rows[i]], axis=1) for i in range(tiles)], axis=0
    )


def iterate(gram_high, gram_low, basis, count):
    def turn(t):
        now = basis[...]
        high, low = halves(now)
        dot = functools.partial(jnp.dot, preferred_element_type=jnp.float32)
        moved = dot(high, gram_high[...]) + dot(low, gram_high[...]) + dot(high, gram_low[...])
        basis[...] = jnp.where(t < count, orthonormal_rows(moved), now)

    pl.loop(0, ITERS)(turn)


def subspace_kernel(rows, frames, count, rank, valid, gram, start, out, high, low, basis):
    high[...] = jnp.zeros_like(high)
    low[...] = jnp.zeros_like(low)
    basis[...] = jnp.zeros_like(basis)
    g_high, g_low = halves(gram[...] * (1.0 / rows))
    high[:frames, :frames] = g_high
    low[:frames, :frames] = g_low
    basis[:, :frames] = start[...]
    iterate(high, low, basis, count[0])
    kept = lax.broadcasted_iota(jnp.int32, basis.shape, 0) < jnp.where(valid[0] > 0, rank[0], 0)
    out[...] = jnp.where(kept, basis[...], 0.0).astype(out.dtype)


def truncated_basis(gram, start, count, rank, valid, rows):
    frames, size = start.shape
    wide = padded(frames)
    smem = pl.BlockSpec(memory_space=pltpu.SMEM)
    vmem = pl.BlockSpec(memory_space=pltpu.VMEM)
    return pl.pallas_call(
        functools.partial(subspace_kernel, rows, frames),
        out_shape=jax.ShapeDtypeStruct((size, wide), jnp.bfloat16),
        in_specs=[smem, smem, smem, vmem, vmem],
        out_specs=vmem,
        scratch_shapes=[
            pltpu.VMEM((wide, wide), jnp.bfloat16),
            pltpu.VMEM((wide, wide), jnp.bfloat16),
            pltpu.VMEM((size, wide), jnp.float32),
        ],
        name="subspace",
    )(count, rank, valid, gram, start.T)


def clutter_kernel(
    rows, chunks, echoes, start, rank_hbm, count_hbm, out,
    gram, sent, got, high, low, basis, mine, other, rank, count, load, sems,
):
    row, col = lax.axis_index("gx"), lax.axis_index("gy")
    cols = lax.axis_size("gy")
    size, frames = start.shape
    wide = gram.shape[1]
    part = echoes.shape[0] // chunks
    small = [
        pltpu.make_async_copy(rank_hbm, rank, load.at[0]),
        pltpu.make_async_copy(count_hbm, count, load.at[1]),
    ]
    for copy in small:
        copy.start()
    partner = (1 - row, col)
    side = 1 - 2 * row
    far = (1 - row, col + side)
    exists = jnp.where(row == 0, col + 1 < cols, col >= 1)
    barrier = pltpu.get_barrier_semaphore()
    pl.semaphore_signal(barrier, inc=1, device_id=partner, device_id_type=MESH)

    @pl.when(exists)
    def _():
        pl.semaphore_signal(barrier, inc=1, device_id=far, device_id_type=MESH)

    def swap(source, target, at, peer):
        return pltpu.make_async_remote_copy(
            src_ref=source,
            dst_ref=target,
            send_sem=sems.at[2 * at],
            recv_sem=sems.at[2 * at + 1],
            device_id=peer,
            device_id_type=MESH,
        )

    high[...] = jnp.zeros_like(high)
    low[...] = jnp.zeros_like(low)
    basis[...] = jnp.zeros_like(basis)
    basis[:, :frames] = start[...]
    gram[...] = jnp.zeros_like(gram)
    total = None
    for i in range(chunks):
        block = echoes[i * part : (i + 1) * part, :]
        term = lax.dot_general(block, block, (((0,), (0,)), ((), ())), preferred_element_type=jnp.float32)
        total = term if total is None else total + term
    for copy in small:
        copy.wait()
    gram[:, :frames] = total
    sent[0] = gram[...].astype(jnp.bfloat16)

    @pl.when(exists)
    def _():
        pl.semaphore_wait(barrier, 2)

    @pl.when(jnp.logical_not(exists))
    def _():
        pl.semaphore_wait(barrier, 1)

    chip = swap(sent.at[0], got.at[0], 0, partner)
    chip.start()
    chip.wait()
    gram[...] = gram[...] + got[0].astype(jnp.float32)
    lane = lax.broadcasted_iota(jnp.int32, gram.shape, 1)
    rank_here = rank[0, 0, 0].astype(jnp.float32)
    count_here = count[0, 0, 0].astype(jnp.float32)
    sent[1] = jnp.where(
        lane == frames, rank_here, jnp.where(lane == frames + 1, count_here, gram[...])
    ).astype(jnp.bfloat16)

    @pl.when(exists)
    def _():
        top = swap(sent.at[1, :LANES, :LANES], got.at[1, :LANES, :LANES], 1, far)
        bottom = swap(sent.at[1, LANES:], got.at[1, LANES:], 3, far)
        top.start()
        bottom.start()
        top.wait()
        bottom.wait()

    @pl.when(jnp.logical_not(exists))
    def _():
        got[1] = jnp.zeros_like(got[1])

    picks = got[1, LANES:, LANES:].astype(jnp.float32)[:SUB, :]
    pick = lambda at, here: jnp.where(
        row == 0, here, jnp.broadcast_to(picks[0:1, frames - LANES + at : frames - LANES + at + 1], basis.shape)
    )
    rank_mine, count_mine = pick(0, rank_here), pick(1, count_here)
    total = jnp.where(lane < frames, gram[...] + got[1].astype(jnp.float32), 0.0) * (1.0 / rows)
    below = jnp.concatenate([total[LANES:, :LANES], jnp.zeros((wide - frames, LANES), jnp.float32)], axis=0)
    pieces = (
        (slice(0, LANES), slice(0, LANES), total[:LANES, :LANES]),
        (slice(LANES, frames), slice(0, wide), total[LANES:, :]),
        (slice(0, LANES), slice(LANES, wide), below.T),
    )
    for at, lanes, piece in pieces:
        g_high, g_low = halves(piece)
        high[at, lanes] = g_high
        low[at, lanes] = g_low
    iterate(high, low, basis, count_mine)
    index = lax.broadcasted_iota(jnp.int32, basis.shape, 0).astype(jnp.float32)
    kept = index < jnp.where(exists, rank_mine, 0.0)
    mine[...] = jnp.where(kept, basis[...], 0.0).astype(mine.dtype)
    pair = swap(mine, other, 2, partner)
    pair.start()
    pair.wait()
    own, theirs = mine[...], other[...]
    out[:size, :] = jnp.where(row == 0, own, theirs)
    out[size:, :] = jnp.where(row == 0, theirs, own)


def clutter_bases(echoes, start, rank, count, voxels):
    frames, size = start.shape
    wide = padded(frames + 2)
    chunks = 4
    anywhere = pl.BlockSpec(memory_space=pl.ANY)
    vmem = pl.BlockSpec(memory_space=pltpu.VMEM)
    square = pltpu.VMEM((wide, wide), jnp.bfloat16)
    return pl.pallas_call(
        functools.partial(clutter_kernel, voxels, chunks),
        out_shape=jax.ShapeDtypeStruct((2 * size, wide), jnp.bfloat16),
        in_specs=[vmem, vmem, anywhere, anywhere],
        out_specs=vmem,
        scratch_shapes=[
            pltpu.VMEM((frames, wide), jnp.float32),
            pltpu.VMEM((2, frames, wide), jnp.bfloat16),
            pltpu.VMEM((2, frames, wide), jnp.bfloat16),
            square,
            square,
            pltpu.VMEM((size, wide), jnp.float32),
            pltpu.VMEM((size, wide), jnp.bfloat16),
            pltpu.VMEM((size, wide), jnp.bfloat16),
            pltpu.SMEM(rank.shape, jnp.int32),
            pltpu.SMEM(count.shape, jnp.int32),
            pltpu.SemaphoreType.DMA((2,)),
            pltpu.SemaphoreType.DMA((8,)),
        ],
        compiler_params=pltpu.CompilerParams(collective_id=0, has_side_effects=True, vmem_limit_bytes=GRANT),
        name="clutter",
    )(echoes, start.T, rank, count)


def project_kernel(span, frames, echoes, vectors, scale_y, scale_x, out):
    base = pl.program_id(0) * (echoes.shape[0] // scale_y.shape[0])
    chunk = scale_y.shape[0]
    q = vectors[:, :frames]
    for part in range(echoes.shape[0] // chunk):
        at = pl.ds(part * chunk, chunk)
        local = echoes[at, :]
        coeff = nt(local, q) * (scale_y[...] * scale_x[pl.ds(base + part, 1), :])
        clutter = jnp.dot(coeff.astype(jnp.bfloat16), q, preferred_element_type=jnp.float32)
        out[at, :] = (local.astype(jnp.float32) - clutter).astype(out.dtype)


def project(echoes, vectors, scale_y, scale_x):
    voxels, frames = echoes.shape
    span = scale_x.shape[0]
    steps = 4
    while span % steps:
        steps //= 2
    whole = lambda a: pl.BlockSpec(a.shape, lambda i: (0, 0))
    return pl.pallas_call(
        functools.partial(project_kernel, span, frames),
        out_shape=jax.ShapeDtypeStruct(echoes.shape, echoes.dtype),
        grid=(steps,),
        in_specs=[
            pl.BlockSpec((voxels // steps, frames), lambda i: (i, 0)),
            whole(vectors),
            whole(scale_y),
            whole(scale_x),
        ],
        out_specs=pl.BlockSpec((voxels // steps, frames), lambda i: (i, 0)),
        name="project",
    )(echoes, vectors, scale_y, scale_x)


def separate_kernel(groups, echoes, vectors, out, result, base, slope, stores):
    span, lines, depth, frames = echoes.shape
    size = vectors.shape[0] // 2
    col, cols = lax.axis_index("gy"), lax.axis_size("gy")
    part = lines // groups
    line = lambda i: pl.ds(i * part, part)
    writes = [pltpu.make_async_copy(result.at[:, line(i)], out.at[:, line(i)], stores.at[i]) for i in range(groups)]
    projector = lambda q: lax.dot_general(q, q, (((0,), (0,)), ((), ())), preferred_element_type=jnp.float32)
    after = projector(vectors[:size, :frames])
    before = projector(vectors[size:, :frames])
    base[...] = before
    slope[...] = after - before
    for i in range(groups):
        for y in range(i * part, i * part + part):
            share = (1.0 + y) / (1.0 + lines)
            share = jnp.where(col == 0, 1.0, jnp.where(col == cols - 1, 0.0, share))
            mixed = (base[...] + share * slope[...]).astype(jnp.bfloat16)
            block = echoes[:, y].reshape(span * depth, frames)
            clutter = jnp.dot(block, mixed, preferred_element_type=jnp.float32)
            rest = (block.astype(jnp.float32) - clutter).astype(out.dtype)
            result[:, y] = rest.reshape(span, depth, frames)
        writes[i].start()
    for copy in writes:
        copy.wait()


def separate(echoes, vectors):
    groups = 4
    frames = echoes.shape[-1]
    anywhere = pl.BlockSpec(memory_space=pl.ANY)
    square = pltpu.VMEM((frames, frames), jnp.float32)
    return pl.pallas_call(
        functools.partial(separate_kernel, groups),
        out_shape=jax.ShapeDtypeStruct(echoes.shape, echoes.dtype),
        in_specs=[pl.BlockSpec(memory_space=pltpu.VMEM)] * 2,
        out_specs=anywhere,
        scratch_shapes=[
            pltpu.VMEM(echoes.shape, echoes.dtype),
            square,
            square,
            pltpu.SemaphoreType.DMA((groups,)),
        ],
        compiler_params=pltpu.CompilerParams(vmem_limit_bytes=GRANT),
        name="separate",
    )(echoes, vectors)


def shares(span, index, count):
    offset = jnp.arange(span, dtype=jnp.float32)
    here = tent(offset, 2.0 * span) * (index <= count - 2).astype(jnp.float32)
    before = tent(offset + span, 2.0 * span) * (index >= 1).astype(jnp.float32)
    return here / (here + before), before / (here + before)


def body(echoes, start, ranks, counts):
    span, _, depth, frames = echoes.shape
    size = start.shape[1]
    row, col = lax.axis_index("gx"), lax.axis_index("gy")
    rows, cols = lax.axis_size("gx"), lax.axis_size("gy")
    flat = echoes.reshape(-1, frames)
    voxels = 4 * flat.shape[0]

    def sent(x, axis, route):
        return lax.ppermute(x, axis, route)

    def basis(total, count, rank, valid):
        return truncated_basis(
            total, start, count.reshape(1), rank.reshape(1), valid.astype(jnp.int32).reshape(1), float(voxels)
        )

    if rows == 2:
        vectors = clutter_bases(flat, start, ranks, counts, float(voxels))
        return separate(echoes, vectors)
    back = lambda n: [(i, i - 1) for i in range(1, n)]
    ahead = lambda n: [(i - 1, i) for i in range(1, n)]
    gram = lax.dot_general(flat, flat, (((0,), (0,)), ((), ())), preferred_element_type=jnp.float32)
    pair = gram + sent(gram.astype(jnp.bfloat16), "gy", back(cols)).astype(jnp.float32)
    total = pair + sent(pair.astype(jnp.bfloat16), "gx", back(rows)).astype(jnp.float32)
    own = basis(total, counts[0, 0, 0], ranks[0, 0, 0], (row <= rows - 2) & (col <= cols - 2))
    left = sent(own, "gy", ahead(cols))
    paired = jnp.concatenate([own, left])
    vectors = jnp.concatenate([paired, sent(paired, "gx", ahead(rows))])
    y_here, y_before = shares(span, col, cols)
    x_here, x_before = shares(span, row, rows)
    scale_ys = [y_here, y_before, y_here, y_before]
    scale_xs = [x_here, x_here, x_before, x_before]
    wide = lambda parts: jnp.concatenate([jnp.broadcast_to(p[:, None], (span, size)) for p in parts], axis=1)
    scale_y = jnp.repeat(wide(scale_ys), depth, axis=0)
    return project(flat, vectors, scale_y, wide(scale_xs)).reshape(echoes.shape)


def solution(mesh):
    placed = (P("gx", "gy", None, None), P(), P("gx", "gy", None), P("gx", "gy", None))
    return jax.shard_map(
        body, mesh=mesh, in_specs=placed, out_specs=P("gx", "gy", None, None), check_vma=False
    )
```

profile of v0, /device:TPU:0, one launch (start us, length us, event | category | flops | bytes accessed | tf_op | source)
XLA Modules:
  0.0 17.4 jit_solution(6925964438296009498)
XLA Ops:
  1.3 0.0 copy-start
  1.3 1.6 %copy-done = bf16[16,16,16,200]{3,2,1,0:T(8,128)(2,1)S(1)} copy-done((bf16[16,16,16,200]{3,2,1,0:T(8,128)(2,1)S(1)}, bf16[16,16,16,200]{3,2,1,0:T(8,128)(2,1)}, u32[]{:S(2)}) %copy-start) | copy-done | bytes 1638424
  2.9 0.0 copy-start.1
  2.9 0.8 %copy-done.1 = f32[200,32]{0,1:T(8,128)S(1)} copy-done((f32[200,32]{0,1:T(8,128)S(1)}, f32[200,32]{0,1:T(8,128)}, u32[]{:S(2)}) %copy-start.1) | copy-done | bytes 25624
  3.6 11.8 %clutter.1.vectors = bf16[64,256]{1,0:T(8,128)(2,1)S(1)} custom-call(bf16[4096,200]{1,0:T(8,128)(2,1)S(1)} %bitcast.2, f32[32,200]{1,0:T(8,128)S(1)} %bitcast.3, s32[1,1,1]{2,1,0:T(1,128)S(6)} %copy.5.rank_hbm, s32[1,1,1]{2,1,0:T(1,128)S(6)} %copy.6.count_hbm), custom_call_target="tpu_custom_call" | custom-call | tf_op jit(solution)/shard_map/clutter/pallas_call | solution.py:243
  15.4 2.0 %separate.1 = bf16[16,16,16,200]{3,2,1,0:T(8,128)(2,1)} custom-call(bf16[16,16,16,200]{3,2,1,0:T(8,128)(2,1)S(1)} %copy-done, bf16[64,256]{1,0:T(8,128)(2,1)S(1)} %clutter.1.vectors), custom_call_target="tpu_custom_call" | custom-call | tf_op jit(solution)/shard_map/separate/pallas_call | solution.py:332
Async XLA Ops:
  1.3 1.6 %copy-start = (bf16[16,16,16,200]{3,2,1,0:T(8,128)(2,1)S(1)}, bf16[16,16,16,200]{3,2,1,0:T(8,128)(2,1)}, u32[]{:S(2)}) copy-start(bf16[16,16,16,200]{3,2,1,0:T(8,128)(2,1)} %echoes.1) | copy-start | bytes 4915204
  2.9 0.8 %copy-start.1 = (f32[200,32]{0,1:T(8,128)S(1)}, f32[200,32]{0,1:T(8,128)}, u32[]{:S(2)}) copy-start(f32[200,32]{0,1:T(8,128)} %param.5) | copy-start | bytes 76804
where the time goes:
time: 17.6 us; the launch traced here: 17.4 us
  Pallas kernels  13.7 us (78%)
  local copies, waits for them, and re-layouts  2.34 us (13%)
  between operations  1.31 us (7%)
    pallas_call x1, Pallas kernels, clutter_bases(): pl.pallas_call(functools.partial(clutter_kernel, voxels, chunks), out_sha...  11.8 us
    unnamed x4, local copies, waits for them, and re-layouts  2.34 us
    pallas_call x1, Pallas kernels, separate(): pl.pallas_call(functools.partial(separate_kernel, groups), out_shape=jax....  1.95 us

commit v1 on v0

--- a/solution.py
+++ b/solution.py
@@ -123,20 +123,21 @@
 
 
 def clutter_kernel(
-    rows, chunks, echoes, start, rank_hbm, count_hbm, out,
-    gram, sent, got, high, low, basis, mine, other, rank, count, load, sems,
+    rows, chunks, echoes_hbm, start_hbm, rank_hbm, count_hbm, out, echoes,
+    gram, sent, got, high, low, basis, mine, other, start, rank, count, load, sems,
 ):
     row, col = lax.axis_index("gx"), lax.axis_index("gy")
     cols = lax.axis_size("gy")
     size, frames = start.shape
     wide = gram.shape[1]
     part = echoes.shape[0] // chunks
+    slab = lambda i: pl.ds(i * part, part)
+    loads = [
+        pltpu.make_async_copy(echoes_hbm.at[slab(i)], echoes.at[slab(i)], load.at[3 + i]) for i in range(chunks)
+    ]
     small = [
-        pltpu.make_async_copy(rank_hbm, rank, load.at[0]),
-        pltpu.make_async_copy(count_hbm, count, load.at[1]),
+        pltpu.make_async_copy(start_hbm, start, load.at[2]),
     ]
-    for copy in small:
-        copy.start()
     partner = (1 - row, col)
     side = 1 - 2 * row
     far = (1 - row, col + side)
@@ -147,6 +148,9 @@
     @pl.when(exists)
     def _():
         pl.semaphore_signal(barrier, inc=1, device_id=far, device_id_type=MESH)
+
+    for copy in loads + small:
+        copy.start()
 
     def swap(source, target, at, peer):
         return pltpu.make_async_remote_copy(
@@ -161,15 +165,16 @@
     high[...] = jnp.zeros_like(high)
     low[...] = jnp.zeros_like(low)
     basis[...] = jnp.zeros_like(basis)
-    basis[:, :frames] = start[...]
     gram[...] = jnp.zeros_like(gram)
     total = None
     for i in range(chunks):
+        loads[i].wait()
         block = echoes[i * part : (i + 1) * part, :]
         term = lax.dot_general(block, block, (((0,), (0,)), ((), ())), preferred_element_type=jnp.float32)
         total = term if total is None else total + term
     for copy in small:
         copy.wait()
+    basis[:, :frames] = start[...]
     gram[:, :frames] = total
     sent[0] = gram[...].astype(jnp.bfloat16)
 
@@ -186,8 +191,8 @@
     chip.wait()
     gram[...] = gram[...] + got[0].astype(jnp.float32)
     lane = lax.broadcasted_iota(jnp.int32, gram.shape, 1)
-    rank_here = rank[0, 0, 0].astype(jnp.float32)
-    count_here = count[0, 0, 0].astype(jnp.float32)
+    rank_here = rank_hbm[0, 0, 0].astype(jnp.float32)
+    count_here = count_hbm[0, 0, 0].astype(jnp.float32)
     sent[1] = jnp.where(
         lane == frames, rank_here, jnp.where(lane == frames + 1, count_here, gram[...])
     ).astype(jnp.bfloat16)
@@ -236,15 +241,18 @@
 def clutter_bases(echoes, start, rank, count, voxels):
     frames, size = start.shape
     wide = padded(frames + 2)
-    chunks = 4
-    anywhere = pl.BlockSpec(memory_space=pl.ANY)
+    chunks = 8
+    hbm = pl.BlockSpec(memory_space=pltpu.HBM)
     vmem = pl.BlockSpec(memory_space=pltpu.VMEM)
     square = pltpu.VMEM((wide, wide), jnp.bfloat16)
     return pl.pallas_call(
         functools.partial(clutter_kernel, voxels, chunks),
-        out_shape=jax.ShapeDtypeStruct((2 * size, wide), jnp.bfloat16),
-        in_specs=[vmem, vmem, anywhere, anywhere],
-        out_specs=vmem,
+        out_shape=[
+            jax.ShapeDtypeStruct((2 * size, wide), jnp.bfloat16),
+            jax.ShapeDtypeStruct(echoes.shape, echoes.dtype),
+        ],
+        in_specs=[hbm] * 2 + [pl.BlockSpec(memory_space=pltpu.SMEM)] * 2,
+        out_specs=[vmem] * 2,
         scratch_shapes=[
             pltpu.VMEM((frames, wide), jnp.float32),
             pltpu.VMEM((2, frames, wide), jnp.bfloat16),
@@ -254,14 +262,15 @@
             pltpu.VMEM((size, wide), jnp.float32),
             pltpu.VMEM((size, wide), jnp.bfloat16),
             pltpu.VMEM((size, wide), jnp.bfloat16),
+            pltpu.VMEM((size, frames), jnp.float32),
             pltpu.SMEM(rank.shape, jnp.int32),
             pltpu.SMEM(count.shape, jnp.int32),
-            pltpu.SemaphoreType.DMA((2,)),
+            pltpu.SemaphoreType.DMA((3 + chunks,)),
             pltpu.SemaphoreType.DMA((8,)),
         ],
         compiler_params=pltpu.CompilerParams(collective_id=0, has_side_effects=True, vmem_limit_bytes=GRANT),
         name="clutter",
-    )(echoes, start.T, rank, count)
+    )(*(pltpu.with_memory_space_constraint(x, pltpu.HBM) for x in (echoes, start.T)), rank, count)
 
 
 def project_kernel(span, frames, echoes, vectors, scale_y, scale_x, out):
@@ -369,8 +378,8 @@
         )
 
     if rows == 2:
-        vectors = clutter_bases(flat, start, ranks, counts, float(voxels))
-        return separate(echoes, vectors)
+        vectors, held = clutter_bases(flat, start, ranks, counts, float(voxels))
+        return separate(held.reshape(echoes.shape), vectors)
     back = lambda n: [(i, i - 1) for i in range(1, n)]
     ahead = lambda n: [(i - 1, i) for i in range(1, n)]
     gram = lax.dot_general(flat, flat, (((0,), (0,)), ((), ())), preferred_element_type=jnp.float32)

time: 17.6 us -> 16.9 us (0.960)
  local copies, waits for them, and re-layouts: 2.34 us -> 0 us
  Pallas kernels: 13.7 us -> 15.5 us
    unnamed x4 -> x0, local copies, waits for them, and re-layouts: 2.34 us -> none
    pallas_call x1, Pallas kernels: 11.8 us -> 13.5 us  [clutter_bases(): pl.pallas_call(functools.partial(clutter_kernel, voxels, chunks), out_sha...]
where the time goes in v1:
time: 16.9 us; the launch traced here: 16.8 us
  Pallas kernels  15.5 us (92%)
  between operations  1.3 us (8%)
    pallas_call x1, Pallas kernels, clutter_bases(): pl.pallas_call(functools.partial(clutter_kernel, voxels, chunks), out_sha...  13.5 us
    pallas_call x1, Pallas kernels, separate(): pl.pallas_call(functools.partial(separate_kernel, groups), out_shape=jax....  1.95 us

profile of v1, /device:TPU:0, one launch (start us, length us, event | category | flops | bytes accessed | tf_op | source)
XLA Modules:
  0.0 16.8 jit_solution(3325367780184406451)
XLA Ops:
  1.3 13.5 %clutter.1 = (bf16[64,256]{1,0:T(8,128)(2,1)S(1)}, bf16[4096,200]{1,0:T(8,128)(2,1)S(1)}) custom-call(bf16[4096,200]{1,0:T(8,128)(2,1)} %bitcast.4, f32[32,200]{1,0:T(8,128)} %bitcast.5, s32[1,1,1]{2,1,0:T(1,128)S(6)} %copy.5.rank_hbm, s32[1,1,1]{2,1,0:T(1,128)S(6)} %copy.6.count_hbm), custom_call_target="tpu_custom_call" | custom-call | tf_op jit(solution)/shard_map/clutter/pallas_call | solution.py:248
  14.8 2.0 %separate.1 = bf16[16,16,16,200]{3,2,1,0:T(8,128)(2,1)} custom-call(bf16[16,16,16,200]{3,2,1,0:T(8,128)(2,1)S(1)} %bitcast.3, bf16[64,256]{1,0:T(8,128)(2,1)S(1)} %get-tuple-element.8.vectors), custom_call_target="tpu_custom_call" | custom-call | tf_op jit(solution)/shard_map/separate/pallas_call | solution.py:341

commit v2 on v1

--- a/solution.py
+++ b/solution.py
@@ -11,6 +11,7 @@
 ITERS = 4
 LANES = 128
 SUB = 8
+BLOCK = 16
 GRANT = 16 << 20
 MESH = pl.DeviceIdType.MESH
 
@@ -37,60 +38,77 @@
     return lax.dot_general(a, b, (((1,), (1,)), ((), ())), preferred_element_type=jnp.float32)
 
 
-def orthonormal_rows(moved):
-    size, width = moved.shape
-    tiles = size // SUB
-    high, low = halves(moved)
-    inner = nt(high, high) + nt(low, high) + nt(high, low)
-    columns = []
-    for j in range(size):
-        first = j // SUB
-        columns.append(
-            [
-                jnp.broadcast_to(inner[SUB * i : SUB * i + SUB, j : j + 1], (SUB, LANES))
-                for i in range(first, tiles)
-            ]
-        )
+def product(high, low, other_high, other_low, dot):
+    size = high.shape[0]
+    both = dot(jnp.concatenate([high, low], axis=0), other_high)
+    return both[:size] + both[size:] + dot(high, other_low)
+
+
+def orthonormal_rows(inner, moved, spare):
+    size = inner.shape[0]
+    tiles, lanes = size // SUB, moved.shape[1] // LANES
     rows = [
-        [moved[SUB * i : SUB * i + SUB, LANES * h : LANES * h + LANES] for h in range(width // LANES)]
-        for i in range(tiles)
+        [moved[SUB * i : SUB * i + SUB, LANES * h : LANES * h + LANES] for h in range(lanes)] for i in range(tiles)
     ]
     place = lax.broadcasted_iota(jnp.int32, (SUB, LANES), 0)
     scales = [None] * tiles
+    spread = lambda x: jnp.broadcast_to(x, (SUB, LANES))
     for k in range(size):
         own, at = k // SUB, k % SUB
-        root = lax.rsqrt(row_of(columns[k][0], at))
+        if k % BLOCK == 0:
+            end = min(k + BLOCK, size)
+            if k == 0:
+                source, base = [inner[SUB * i : SUB * i + SUB] for i in range(tiles)], 0
+            else:
+                source, base = [r[spare // LANES] for r in rows], spare % LANES
+            columns = {
+                j: {i: spread(source[i][:, base + j : base + j + 1]) for i in range(j // SUB, tiles)}
+                for j in range(k, end)
+            }
+            pivot = row_of(columns[k][own], at)
+        root = lax.rsqrt(pivot)
         scales[own] = root if at == 0 else jnp.where(place == at, root, scales[own])
         if k == size - 1:
             break
         inverse = root * root
-        factor = [c * inverse for c in columns[k]]
-        factor[0] = jnp.where(place > at, factor[0], 0.0)
-        for j in range(k + 1, size):
-            pivot = row_of(columns[k][j // SUB - own], j % SUB)
-            shift = j // SUB - own
-            columns[j] = [c - factor[i + shift] * pivot for i, c in enumerate(columns[j])]
-        for h in range(width // LANES):
-            pivot = row_of(rows[own][h], at)
+        lines = {j: row_of(columns[k][j // SUB], j % SUB) for j in range(k + 1, end)}
+        if k + 1 < end:
+            pivot = row_of(columns[k + 1][(k + 1) // SUB], (k + 1) % SUB) - lines[k + 1] * lines[k + 1] * inverse
+        factor = {i: c * inverse for i, c in columns[k].items()}
+        factor[own] = jnp.where(place > at, factor[own], 0.0)
+        for j in range(k + 1, end):
+            columns[j] = {i: c - factor[i] * lines[j] for i, c in columns[j].items()}
+        for h in reversed(range(lanes)):
+            line = row_of(rows[own][h], at)
             for i in range(own if at < SUB - 1 else own + 1, tiles):
-                rows[i][h] = rows[i][h] - factor[i - own] * pivot
+                rows[i][h] = rows[i][h] - factor[i] * line
     return jnp.concatenate(
         [jnp.concatenate([part * scales[i] for part in rows[i]], axis=1) for i in range(tiles)], axis=0
     )
 
 
-def iterate(gram_high, gram_low, basis, count):
+def iterate(gram_high, gram_low, moved, basis, count, frames):
+    size, wide = basis.shape
+    spare = -(-frames // 16) * 16
+    own = slice(spare, spare + size)
+    moved[...] = product(*halves(basis[...]), gram_high[...], gram_low[...], nt)
+
     def turn(t):
-        now = basis[...]
+        now = moved[...]
         high, low = halves(now)
-        dot = functools.partial(jnp.dot, preferred_element_type=jnp.float32)
-        moved = dot(high, gram_high[...]) + dot(low, gram_high[...]) + dot(high, gram_low[...])
-        basis[...] = jnp.where(t < count, orthonormal_rows(moved), now)
+        gram_high[own, :] = high
+        gram_low[own, :] = low
+        inner = product(high, low, high, low, nt)
+        ahead = product(high, low, gram_high[...], gram_low[...], nt)
+        both = orthonormal_rows(inner, jnp.concatenate([now, ahead], axis=1), wide + spare)
+        basis[...] = jnp.where(t < count, both[:, :wide], basis[...])
+        lane = lax.broadcasted_iota(jnp.int32, now.shape, 1)
+        moved[...] = jnp.where(lane < frames, both[:, wide:], 0.0)
 
     pl.loop(0, ITERS)(turn)
 
 
-def subspace_kernel(rows, frames, count, rank, valid, gram, start, out, high, low, basis):
+def subspace_kernel(rows, frames, count, rank, valid, gram, start, out, high, low, moved, basis):
     high[...] = jnp.zeros_like(high)
     low[...] = jnp.zeros_like(low)
     basis[...] = jnp.zeros_like(basis)
@@ -98,7 +116,7 @@
     high[:frames, :frames] = g_high
     low[:frames, :frames] = g_low
     basis[:, :frames] = start[...]
-    iterate(high, low, basis, count[0])
+    iterate(high, low, moved, basis, count[0], frames)
     kept = lax.broadcasted_iota(jnp.int32, basis.shape, 0) < jnp.where(valid[0] > 0, rank[0], 0)
     out[...] = jnp.where(kept, basis[...], 0.0).astype(out.dtype)
 
@@ -117,14 +135,55 @@
             pltpu.VMEM((wide, wide), jnp.bfloat16),
             pltpu.VMEM((wide, wide), jnp.bfloat16),
             pltpu.VMEM((size, wide), jnp.float32),
+            pltpu.VMEM((size, wide), jnp.float32),
         ],
         name="subspace",
     )(count, rank, valid, gram, start.T)
 
 
+def folded(gram):
+    half, rest = LANES // 2, gram.shape[0] - LANES
+    corner = pltpu.roll(gram[:half, :LANES], half, 1)
+    lane = lax.broadcasted_iota(jnp.int32, corner.shape, 1)
+    return jnp.concatenate(
+        [
+            gram[half:LANES, :LANES],
+            gram[LANES:, :LANES],
+            jnp.where(lane < half, gram[LANES : LANES + half, LANES:], corner),
+            gram[LANES + half :, LANES:],
+        ],
+        axis=0,
+    )
+
+
+def unfolded(packed, rest):
+    half = LANES // 2
+    lower, cross = packed[:half], packed[half : half + rest]
+    square, strip = packed[half + rest : LANES + rest], packed[LANES + rest :]
+    lane = lax.broadcasted_iota(jnp.int32, square.shape, 1)
+    filled = lambda above, x, below: jnp.concatenate(
+        [jnp.zeros((n, LANES), jnp.float32) if isinstance(n, int) else n for n in (above, x, below) if not isinstance(n, int) or n],
+        axis=0,
+    )
+    upper = filled(half, lower, 0).T
+    side = filled(half, strip, half - strip.shape[0]).T
+    first = jnp.where(lane < half, pltpu.roll(square, half, 1), upper[:half])
+    mixed = jnp.where(lane < half, square, jnp.where(lane < rest, side[:half], 0.0))
+    tail = jnp.where(lax.broadcasted_iota(jnp.int32, strip.shape, 1) < rest, strip, 0.0)
+    here, there = slice(0, LANES), slice(LANES, 2 * LANES)
+    return (
+        (slice(0, half), here, first),
+        (slice(half, LANES), here, lower),
+        (slice(LANES, LANES + rest), here, cross),
+        (slice(0, LANES), there, filled(0, cross, LANES - rest).T),
+        (slice(LANES, LANES + half), there, mixed),
+        (slice(LANES + half, LANES + rest), there, tail),
+    )
+
+
 def clutter_kernel(
     rows, chunks, echoes_hbm, start_hbm, rank_hbm, count_hbm, out, echoes,
-    gram, sent, got, high, low, basis, mine, other, start, rank, count, load, sems,
+    gram, sent, got, high, low, moved, basis, mine, other, start, rank, count, load, sems,
 ):
     row, col = lax.axis_index("gx"), lax.axis_index("gy")
     cols = lax.axis_size("gy")
@@ -176,7 +235,8 @@
         copy.wait()
     basis[:, :frames] = start[...]
     gram[:, :frames] = total
-    sent[0] = gram[...].astype(jnp.bfloat16)
+    mine_sum = folded(gram)
+    sent[0] = mine_sum.astype(jnp.bfloat16)
 
     @pl.when(exists)
     def _():
@@ -189,44 +249,34 @@
     chip = swap(sent.at[0], got.at[0], 0, partner)
     chip.start()
     chip.wait()
-    gram[...] = gram[...] + got[0].astype(jnp.float32)
-    lane = lax.broadcasted_iota(jnp.int32, gram.shape, 1)
+    chip_sum = mine_sum + got[0].astype(jnp.float32)
     rank_here = rank_hbm[0, 0, 0].astype(jnp.float32)
     count_here = count_hbm[0, 0, 0].astype(jnp.float32)
-    sent[1] = jnp.where(
-        lane == frames, rank_here, jnp.where(lane == frames + 1, count_here, gram[...])
-    ).astype(jnp.bfloat16)
+    rest = frames - LANES
+    lane = lax.broadcasted_iota(jnp.int32, (SUB, LANES), 1)
+    strip = jnp.where(lane == rest, rank_here, jnp.where(lane == rest + 1, count_here, chip_sum[-SUB:]))
+    sent[1] = jnp.concatenate([chip_sum[:-SUB], strip], axis=0).astype(jnp.bfloat16)
 
     @pl.when(exists)
     def _():
-        top = swap(sent.at[1, :LANES, :LANES], got.at[1, :LANES, :LANES], 1, far)
-        bottom = swap(sent.at[1, LANES:], got.at[1, LANES:], 3, far)
-        top.start()
-        bottom.start()
-        top.wait()
-        bottom.wait()
+        over = swap(sent.at[1], got.at[1], 1, far)
+        over.start()
+        over.wait()
 
     @pl.when(jnp.logical_not(exists))
     def _():
         got[1] = jnp.zeros_like(got[1])
 
-    picks = got[1, LANES:, LANES:].astype(jnp.float32)[:SUB, :]
+    theirs = got[1].astype(jnp.float32)
     pick = lambda at, here: jnp.where(
-        row == 0, here, jnp.broadcast_to(picks[0:1, frames - LANES + at : frames - LANES + at + 1], basis.shape)
+        row == 0, here, jnp.broadcast_to(theirs[-SUB : -SUB + 1, rest + at : rest + at + 1], basis.shape)
     )
     rank_mine, count_mine = pick(0, rank_here), pick(1, count_here)
-    total = jnp.where(lane < frames, gram[...] + got[1].astype(jnp.float32), 0.0) * (1.0 / rows)
-    below = jnp.concatenate([total[LANES:, :LANES], jnp.zeros((wide - frames, LANES), jnp.float32)], axis=0)
-    pieces = (
-        (slice(0, LANES), slice(0, LANES), total[:LANES, :LANES]),
-        (slice(LANES, frames), slice(0, wide), total[LANES:, :]),
-        (slice(0, LANES), slice(LANES, wide), below.T),
-    )
-    for at, lanes, piece in pieces:
+    for at, lanes, piece in unfolded((chip_sum + theirs) * (1.0 / rows), rest):
         g_high, g_low = halves(piece)
         high[at, lanes] = g_high
         low[at, lanes] = g_low
-    iterate(high, low, basis, count_mine)
+    iterate(high, low, moved, basis, count_mine, frames)
     index = lax.broadcasted_iota(jnp.int32, basis.shape, 0).astype(jnp.float32)
     kept = index < jnp.where(exists, rank_mine, 0.0)
     mine[...] = jnp.where(kept, basis[...], 0.0).astype(mine.dtype)
@@ -241,7 +291,7 @@
 def clutter_bases(echoes, start, rank, count, voxels):
     frames, size = start.shape
     wide = padded(frames + 2)
-    chunks = 8
+    chunks = 2
     hbm = pl.BlockSpec(memory_space=pltpu.HBM)
     vmem = pl.BlockSpec(memory_space=pltpu.VMEM)
     square = pltpu.VMEM((wide, wide), jnp.bfloat16)
@@ -255,10 +305,11 @@
         out_specs=[vmem] * 2,
         scratch_shapes=[
             pltpu.VMEM((frames, wide), jnp.float32),
-            pltpu.VMEM((2, frames, wide), jnp.bfloat16),
-            pltpu.VMEM((2, frames, wide), jnp.bfloat16),
+            pltpu.VMEM((2, 2 * frames - 3 * LANES // 2, LANES), jnp.bfloat16),
+            pltpu.VMEM((2, 2 * frames - 3 * LANES // 2, LANES), jnp.bfloat16),
             square,
             square,
+            pltpu.VMEM((size, wide), jnp.float32),
             pltpu.VMEM((size, wide), jnp.float32),
             pltpu.VMEM((size, wide), jnp.bfloat16),
             pltpu.VMEM((size, wide), jnp.bfloat16),

time: 16.9 us -> 15.9 us (0.941)
  Pallas kernels: 15.5 us -> 14.5 us
    pallas_call x1, Pallas kernels: 13.5 us -> 12.5 us  [clutter_bases(): pl.pallas_call(functools.partial(clutter_kernel, voxels, chunks), out_sha...]
where the time goes in v2:
time: 15.9 us; the launch traced here: 15.8 us
  Pallas kernels  14.5 us (91%)
  between operations  1.3 us (8%)
    pallas_call x1, Pallas kernels, clutter_bases(): pl.pallas_call(functools.partial(clutter_kernel, voxels, chunks), out_sha...  12.5 us
    pallas_call x1, Pallas kernels, separate(): pl.pallas_call(functools.partial(separate_kernel, groups), out_shape=jax....  1.95 us

profile of v2, /device:TPU:0, one launch (start us, length us, event | category | flops | bytes accessed | tf_op | source)
XLA Modules:
  0.0 15.8 jit_solution(17163254723274948090)
XLA Ops:
  1.3 12.5 %clutter.1 = (bf16[64,256]{1,0:T(8,128)(2,1)S(1)}, bf16[4096,200]{1,0:T(8,128)(2,1)S(1)}) custom-call(bf16[4096,200]{1,0:T(8,128)(2,1)} %bitcast.4, f32[32,200]{1,0:T(8,128)} %bitcast.5, s32[1,1,1]{2,1,0:T(1,128)S(6)} %copy.5.rank_hbm, s32[1,1,1]{2,1,0:T(1,128)S(6)} %copy.6.count_hbm), custom_call_target="tpu_custom_call" | custom-call | tf_op jit(solution)/shard_map/clutter/pallas_call | solution.py:298
  13.8 2.0 %separate.1 = bf16[16,16,16,200]{3,2,1,0:T(8,128)(2,1)} custom-call(bf16[16,16,16,200]{3,2,1,0:T(8,128)(2,1)S(1)} %bitcast.3, bf16[64,256]{1,0:T(8,128)(2,1)S(1)} %get-tuple-element.8.vectors), custom_call_target="tpu_custom_call" | custom-call | tf_op jit(solution)/shard_map/separate/pallas_call | solution.py:392

commit v3 on v2

--- a/solution.py
+++ b/solution.py
@@ -12,6 +12,7 @@
 LANES = 128
 SUB = 8
 BLOCK = 16
+HEAD = 16
 GRANT = 16 << 20
 MESH = pl.DeviceIdType.MESH
 
@@ -183,7 +184,7 @@
 
 def clutter_kernel(
     rows, chunks, echoes_hbm, start_hbm, rank_hbm, count_hbm, out, echoes,
-    gram, sent, got, high, low, moved, basis, mine, other, start, rank, count, load, sems,
+    gram, sent, got, early, high, low, moved, basis, mine, other, start, rank, count, load, sems,
 ):
     row, col = lax.axis_index("gx"), lax.axis_index("gy")
     cols = lax.axis_size("gy")
@@ -200,13 +201,24 @@
     partner = (1 - row, col)
     side = 1 - 2 * row
     far = (1 - row, col + side)
-    exists = jnp.where(row == 0, col + 1 < cols, col >= 1)
+    before, after = col >= 1, col + 1 < cols
+    exists = jnp.where(row == 0, after, before)
+    down, up = (0, col - 1), (1, col + 1)
     barrier = pltpu.get_barrier_semaphore()
-    pl.semaphore_signal(barrier, inc=1, device_id=partner, device_id_type=MESH)
+    meet = lambda peer: pl.semaphore_signal(barrier, inc=1, device_id=peer, device_id_type=MESH)
+    meet(partner)
+
+    @pl.when(before)
+    def _():
+        meet(down)
+
+    @pl.when(after)
+    def _():
+        meet(up)
 
     @pl.when(exists)
     def _():
-        pl.semaphore_signal(barrier, inc=1, device_id=far, device_id_type=MESH)
+        meet((row, col + side))
 
     for copy in loads + small:
         copy.start()
@@ -238,16 +250,29 @@
     mine_sum = folded(gram)
     sent[0] = mine_sum.astype(jnp.bfloat16)
 
-    @pl.when(exists)
-    def _():
-        pl.semaphore_wait(barrier, 2)
-
-    @pl.when(jnp.logical_not(exists))
-    def _():
-        pl.semaphore_wait(barrier, 1)
-
+    pl.semaphore_wait(barrier, 1 + jnp.where(before, 1 + row, 0) + jnp.where(after, 2 - row, 0))
     chip = swap(sent.at[0], got.at[0], 0, partner)
     chip.start()
+    head = early.shape[1]
+
+    def hand(at, peer):
+        return pltpu.make_async_remote_copy(
+            src_ref=sent.at[0, :head],
+            dst_ref=early.at[row],
+            send_sem=sems.at[6 + at],
+            recv_sem=sems.at[8 + row],
+            device_id=peer,
+            device_id_type=MESH,
+        )
+
+    @pl.when(before)
+    def _():
+        hand(0, down).start()
+
+    @pl.when(after)
+    def _():
+        hand(1, up).start()
+
     chip.wait()
     chip_sum = mine_sum + got[0].astype(jnp.float32)
     rank_here = rank_hbm[0, 0, 0].astype(jnp.float32)
@@ -259,15 +284,27 @@
 
     @pl.when(exists)
     def _():
-        over = swap(sent.at[1], got.at[1], 1, far)
+        over = swap(sent.at[1, head:], got.at[1, head:], 1, far)
         over.start()
+        for at in range(2):
+            pltpu.make_async_remote_copy(
+                src_ref=sent.at[0, :head],
+                dst_ref=early.at[at],
+                send_sem=sems.at[6],
+                recv_sem=sems.at[8 + at],
+                device_id=far,
+                device_id_type=MESH,
+            ).wait_recv()
         over.wait()
 
     @pl.when(jnp.logical_not(exists))
     def _():
-        got[1] = jnp.zeros_like(got[1])
-
-    theirs = got[1].astype(jnp.float32)
+        got[1, head:] = jnp.zeros_like(got[1, head:])
+        early[...] = jnp.zeros_like(early)
+
+    theirs = jnp.concatenate(
+        [early[0].astype(jnp.float32) + early[1].astype(jnp.float32), got[1, head:].astype(jnp.float32)], axis=0
+    )
     pick = lambda at, here: jnp.where(
         row == 0, here, jnp.broadcast_to(theirs[-SUB : -SUB + 1, rest + at : rest + at + 1], basis.shape)
     )
@@ -282,6 +319,15 @@
     mine[...] = jnp.where(kept, basis[...], 0.0).astype(mine.dtype)
     pair = swap(mine, other, 2, partner)
     pair.start()
+
+    @pl.when(before)
+    def _():
+        hand(0, down).wait_send()
+
+    @pl.when(after)
+    def _():
+        hand(1, up).wait_send()
+
     pair.wait()
     own, theirs = mine[...], other[...]
     out[:size, :] = jnp.where(row == 0, own, theirs)
@@ -307,6 +353,7 @@
             pltpu.VMEM((frames, wide), jnp.float32),
             pltpu.VMEM((2, 2 * frames - 3 * LANES // 2, LANES), jnp.bfloat16),
             pltpu.VMEM((2, 2 * frames - 3 * LANES // 2, LANES), jnp.bfloat16),
+            pltpu.VMEM((2, (2 * frames - 3 * LANES // 2) // 32 * HEAD, LANES), jnp.bfloat16),
             square,
             square,
             pltpu.VMEM((size, wide), jnp.float32),
@@ -317,7 +364,7 @@
             pltpu.SMEM(rank.shape, jnp.int32),
             pltpu.SMEM(count.shape, jnp.int32),
             pltpu.SemaphoreType.DMA((3 + chunks,)),
-            pltpu.SemaphoreType.DMA((8,)),
+            pltpu.SemaphoreType.DMA((10,)),
         ],
         compiler_params=pltpu.CompilerParams(collective_id=0, has_side_effects=True, vmem_limit_bytes=GRANT),
         name="clutter",
@@ -385,7 +432,7 @@
 
 
 def separate(echoes, vectors):
-    groups = 4
+    groups = 8
     frames = echoes.shape[-1]
     anywhere = pl.BlockSpec(memory_space=pl.ANY)
     square = pltpu.VMEM((frames, frames), jnp.float32)

time: 15.9 us -> 15.4 us (0.969)
  Pallas kernels: 14.5 us -> 14 us
    pallas_call x1, Pallas kernels: 12.5 us -> 12.1 us  [clutter_bases(): pl.pallas_call(functools.partial(clutter_kernel, voxels, chunks), out_sha...]
where the time goes in v3:
time: 15.4 us; the launch traced here: 15.3 us
  Pallas kernels  14 us (91%)
  between operations  1.3 us (8%)
    pallas_call x1, Pallas kernels, clutter_bases(): pl.pallas_call(functools.partial(clutter_kernel, voxels, chunks), out_sha...  12.1 us
    pallas_call x1, Pallas kernels, separate(): pl.pallas_call(functools.partial(separate_kernel, groups), out_shape=jax....  1.9 us

profile of v3, /device:TPU:0, one launch (start us, length us, event | category | flops | bytes accessed | tf_op | source)
XLA Modules:
  0.0 15.3 jit_solution(7842831250599255652)
XLA Ops:
  1.3 12.1 %clutter.1 = (bf16[64,256]{1,0:T(8,128)(2,1)S(1)}, bf16[4096,200]{1,0:T(8,128)(2,1)S(1)}) custom-call(bf16[4096,200]{1,0:T(8,128)(2,1)} %bitcast.4, f32[32,200]{1,0:T(8,128)} %bitcast.5, s32[1,1,1]{2,1,0:T(1,128)S(6)} %copy.5.rank_hbm, s32[1,1,1]{2,1,0:T(1,128)S(6)} %copy.6.count_hbm), custom_call_target="tpu_custom_call" | custom-call | tf_op jit(solution)/shard_map/clutter/pallas_call | solution.py:344
  13.4 1.9 %separate.1 = bf16[16,16,16,200]{3,2,1,0:T(8,128)(2,1)} custom-call(bf16[16,16,16,200]{3,2,1,0:T(8,128)(2,1)S(1)} %bitcast.3, bf16[64,256]{1,0:T(8,128)(2,1)S(1)} %get-tuple-element.8.vectors), custom_call_target="tpu_custom_call" | custom-call | tf_op jit(solution)/shard_map/separate/pallas_call | solution.py:439

commit v4 on v3

--- a/solution.py
+++ b/solution.py
@@ -66,6 +66,7 @@
                 j: {i: spread(source[i][:, base + j : base + j + 1]) for i in range(j // SUB, tiles)}
                 for j in range(k, end)
             }
+            columns[k] = {i: jnp.where(place >= 0, c, 0.0) for i, c in columns[k].items()}
             pivot = row_of(columns[k][own], at)
         root = lax.rsqrt(pivot)
         scales[own] = root if at == 0 else jnp.where(place == at, root, scales[own])
@@ -88,28 +89,29 @@
     )
 
 
-def iterate(gram_high, gram_low, moved, basis, count, frames):
+def iterate(gram_high, gram_low, basis, count, frames):
     size, wide = basis.shape
     spare = -(-frames // 16) * 16
     own = slice(spare, spare + size)
-    moved[...] = product(*halves(basis[...]), gram_high[...], gram_low[...], nt)
+    basis[...] = product(*halves(basis[...]), gram_high[...], gram_low[...], nt)
+    lane = lax.broadcasted_iota(jnp.int32, basis.shape, 1)
 
     def turn(t):
-        now = moved[...]
+        now = basis[...]
         high, low = halves(now)
         gram_high[own, :] = high
         gram_low[own, :] = low
         inner = product(high, low, high, low, nt)
         ahead = product(high, low, gram_high[...], gram_low[...], nt)
-        both = orthonormal_rows(inner, jnp.concatenate([now, ahead], axis=1), wide + spare)
-        basis[...] = jnp.where(t < count, both[:, :wide], basis[...])
-        lane = lax.broadcasted_iota(jnp.int32, now.shape, 1)
-        moved[...] = jnp.where(lane < frames, both[:, wide:], 0.0)
+        last = t == ITERS - 1
+        rows = jnp.where((lane < frames) & last, now, ahead)
+        done = orthonormal_rows(inner, rows, spare)
+        basis[...] = jnp.where(lane < frames, jnp.where((t + 1 < count) | last, done, now), 0.0)
 
     pl.loop(0, ITERS)(turn)
 
 
-def subspace_kernel(rows, frames, count, rank, valid, gram, start, out, high, low, moved, basis):
+def subspace_kernel(rows, frames, count, rank, valid, gram, start, out, high, low, basis):
     high[...] = jnp.zeros_like(high)
     low[...] = jnp.zeros_like(low)
     basis[...] = jnp.zeros_like(basis)
@@ -117,7 +119,7 @@
     high[:frames, :frames] = g_high
     low[:frames, :frames] = g_low
     basis[:, :frames] = start[...]
-    iterate(high, low, moved, basis, count[0], frames)
+    iterate(high, low, basis, count[0], frames)
     kept = lax.broadcasted_iota(jnp.int32, basis.shape, 0) < jnp.where(valid[0] > 0, rank[0], 0)
     out[...] = jnp.where(kept, basis[...], 0.0).astype(out.dtype)
 
@@ -136,7 +138,6 @@
             pltpu.VMEM((wide, wide), jnp.bfloat16),
             pltpu.VMEM((wide, wide), jnp.bfloat16),
             pltpu.VMEM((size, wide), jnp.float32),
-            pltpu.VMEM((size, wide), jnp.float32),
         ],
         name="subspace",
     )(count, rank, valid, gram, start.T)
@@ -184,16 +185,18 @@
 
 def clutter_kernel(
     rows, chunks, echoes_hbm, start_hbm, rank_hbm, count_hbm, out, echoes,
-    gram, sent, got, early, high, low, moved, basis, mine, other, start, rank, count, load, sems,
+    gram, sent, got, early, high, low, basis, mine, other, start, rank, count, load, sems,
 ):
     row, col = lax.axis_index("gx"), lax.axis_index("gy")
     cols = lax.axis_size("gy")
     size, frames = start.shape
     wide = gram.shape[1]
     part = echoes.shape[0] // chunks
-    slab = lambda i: pl.ds(i * part, part)
+    pieces = echoes.shape[0] // (load.shape[0] - 3)
+    slab = lambda i: pl.ds(i * pieces, pieces)
     loads = [
-        pltpu.make_async_copy(echoes_hbm.at[slab(i)], echoes.at[slab(i)], load.at[3 + i]) for i in range(chunks)
+        pltpu.make_async_copy(echoes_hbm.at[slab(i)], echoes.at[slab(i)], load.at[3 + i])
+        for i in range(load.shape[0] - 3)
     ]
     small = [
         pltpu.make_async_copy(start_hbm, start, load.at[2]),
@@ -239,7 +242,8 @@
     gram[...] = jnp.zeros_like(gram)
     total = None
     for i in range(chunks):
-        loads[i].wait()
+        for copy in loads[i * len(loads) // chunks : (i + 1) * len(loads) // chunks]:
+            copy.wait()
         block = echoes[i * part : (i + 1) * part, :]
         term = lax.dot_general(block, block, (((0,), (0,)), ((), ())), preferred_element_type=jnp.float32)
         total = term if total is None else total + term
@@ -313,7 +317,7 @@
         g_high, g_low = halves(piece)
         high[at, lanes] = g_high
         low[at, lanes] = g_low
-    iterate(high, low, moved, basis, count_mine, frames)
+    iterate(high, low, basis, count_mine, frames)
     index = lax.broadcasted_iota(jnp.int32, basis.shape, 0).astype(jnp.float32)
     kept = index < jnp.where(exists, rank_mine, 0.0)
     mine[...] = jnp.where(kept, basis[...], 0.0).astype(mine.dtype)
@@ -357,13 +361,12 @@
             square,
             square,
             pltpu.VMEM((size, wide), jnp.float32),
-            pltpu.VMEM((size, wide), jnp.float32),
             pltpu.VMEM((size, wide), jnp.bfloat16),
             pltpu.VMEM((size, wide), jnp.bfloat16),
             pltpu.VMEM((size, frames), jnp.float32),
             pltpu.SMEM(rank.shape, jnp.int32),
             pltpu.SMEM(count.shape, jnp.int32),
-            pltpu.SemaphoreType.DMA((3 + chunks,)),
+            pltpu.SemaphoreType.DMA((3 + 4,)),
             pltpu.SemaphoreType.DMA((10,)),
         ],
         compiler_params=pltpu.CompilerParams(collective_id=0, has_side_effects=True, vmem_limit_bytes=GRANT),

time: 15.4 us -> 15.4 us (level)
  no operation moved by 1% of the time
where the time goes in v4:
time: 15.4 us; the launch traced here: 15.2 us
  Pallas kernels  13.9 us (90%)
  between operations  1.3 us (8%)
    pallas_call x1, Pallas kernels, clutter_bases(): pl.pallas_call(functools.partial(clutter_kernel, voxels, chunks), out_sha...  12 us
    pallas_call x1, Pallas kernels, separate(): pl.pallas_call(functools.partial(separate_kernel, groups), out_shape=jax....  1.91 us

profile of v4, /device:TPU:0, one launch (start us, length us, event | category | flops | bytes accessed | tf_op | source)
XLA Modules:
  0.0 15.2 jit_solution(6572583715463442733)
XLA Ops:
  1.3 12.0 %clutter.1 = (bf16[64,256]{1,0:T(8,128)(2,1)S(1)}, bf16[4096,200]{1,0:T(8,128)(2,1)S(1)}) custom-call(bf16[4096,200]{1,0:T(8,128)(2,1)} %bitcast.4, f32[32,200]{1,0:T(8,128)} %bitcast.5, s32[1,1,1]{2,1,0:T(1,128)S(6)} %copy.5.rank_hbm, s32[1,1,1]{2,1,0:T(1,128)S(6)} %copy.6.count_hbm), custom_call_target="tpu_custom_call" | custom-call | tf_op jit(solution)/shard_map/clutter/pallas_call | solution.py:348
  13.3 1.9 %separate.1 = bf16[16,16,16,200]{3,2,1,0:T(8,128)(2,1)} custom-call(bf16[16,16,16,200]{3,2,1,0:T(8,128)(2,1)S(1)} %bitcast.3, bf16[64,256]{1,0:T(8,128)(2,1)S(1)} %get-tuple-element.8.vectors), custom_call_target="tpu_custom_call" | custom-call | tf_op jit(solution)/shard_map/separate/pallas_call | solution.py:442

commit v5 on v4

--- a/solution.py
+++ b/solution.py
@@ -418,16 +418,16 @@
     projector = lambda q: lax.dot_general(q, q, (((0,), (0,)), ((), ())), preferred_element_type=jnp.float32)
     after = projector(vectors[:size, :frames])
     before = projector(vectors[size:, :frames])
-    base[...] = before
-    slope[...] = after - before
+    diagonal = lax.broadcasted_iota(jnp.int32, base.shape, 0) == lax.broadcasted_iota(jnp.int32, base.shape, 1)
+    base[...] = jnp.where(diagonal, 1.0, 0.0) - before
+    slope[...] = before - after
     for i in range(groups):
         for y in range(i * part, i * part + part):
             share = (1.0 + y) / (1.0 + lines)
             share = jnp.where(col == 0, 1.0, jnp.where(col == cols - 1, 0.0, share))
             mixed = (base[...] + share * slope[...]).astype(jnp.bfloat16)
             block = echoes[:, y].reshape(span * depth, frames)
-            clutter = jnp.dot(block, mixed, preferred_element_type=jnp.float32)
-            rest = (block.astype(jnp.float32) - clutter).astype(out.dtype)
+            rest = jnp.dot(block, mixed, preferred_element_type=jnp.float32).astype(out.dtype)
             result[:, y] = rest.reshape(span, depth, frames)
         writes[i].start()
     for copy in writes:

time: 15.4 us -> 15.3 us (level)
  no operation moved by 1% of the time
where the time goes in v5:
time: 15.3 us; the launch traced here: 15.1 us
  Pallas kernels  13.8 us (90%)
  between operations  1.3 us (8%)
    pallas_call x1, Pallas kernels, clutter_bases(): pl.pallas_call(functools.partial(clutter_kernel, voxels, chunks), out_sha...  12 us
    pallas_call x1, Pallas kernels, separate(): pl.pallas_call(functools.partial(separate_kernel, groups), out_shape=jax....  1.84 us

profile of v5, /device:TPU:0, one launch (start us, length us, event | category | flops | bytes accessed | tf_op | source)
XLA Modules:
  0.0 15.1 jit_solution(8544331893697435231)
XLA Ops:
  1.3 12.0 %clutter.1 = (bf16[64,256]{1,0:T(8,128)(2,1)S(1)}, bf16[4096,200]{1,0:T(8,128)(2,1)S(1)}) custom-call(bf16[4096,200]{1,0:T(8,128)(2,1)} %bitcast.4, f32[32,200]{1,0:T(8,128)} %bitcast.5, s32[1,1,1]{2,1,0:T(1,128)S(6)} %copy.5.rank_hbm, s32[1,1,1]{2,1,0:T(1,128)S(6)} %copy.6.count_hbm), custom_call_target="tpu_custom_call" | custom-call | tf_op jit(solution)/shard_map/clutter/pallas_call | solution.py:348
  13.3 1.8 %separate.1 = bf16[16,16,16,200]{3,2,1,0:T(8,128)(2,1)} custom-call(bf16[16,16,16,200]{3,2,1,0:T(8,128)(2,1)S(1)} %bitcast.3, bf16[64,256]{1,0:T(8,128)(2,1)S(1)} %get-tuple-element.8.vectors), custom_call_target="tpu_custom_call" | custom-call | tf_op jit(solution)/shard_map/separate/pallas_call | solution.py:442
